TPU v7x, 32 devices: a whole 2x2x4 slice. The times are simulated.
32 devices in a mesh: dp: 8 (over z, y), neg: 4 (over x, core).
Axes of the slice: x: 2, y: 2, z: 4, core: 2. Of those that a mesh axis runs over, the one named last changes fastest.
Arguments:
- query_features: bfloat16 [8192, 512], P(('dp', 'neg')), may hold values from -8 to 8
- positive_features: bfloat16 [8192, 512], P(('dp', 'neg')), may hold values from -6 to 6
- negative_features: bfloat16 [16384, 512], P(('neg', 'dp')), may hold values from -6 to 6
- positive_ids: int32 [8192], P('dp'), may hold values from 0 to 8191, as said below
- positive_counts: int32 [8192], P(('dp', 'neg')), may hold values from 1 to 16
- negative_ids: int32 [16384], P('neg'), may hold values from 0 to 4095, as said below
- negative_counts: int32 [16384], P('neg'), may hold values from 64 to 4096
- query_first: bfloat16 [512, 1024], replicated, may hold values from -0.25 to 0.25
- query_second: bfloat16 [1024, 512], replicated, may hold values from -0.1875 to 0.1875
- query_third: bfloat16 [512, 256], replicated, may hold values from -0.25 to 0.25
- item_first: bfloat16 [512, 1024], replicated, may hold values from -0.25 to 0.25
- item_second: bfloat16 [1024, 512], replicated, may hold values from -0.1875 to 0.1875
- item_third: bfloat16 [512, 256], replicated, may hold values from -0.25 to 0.25
Outputs:
- mean_loss: float32 [], replicated
- clipped_query_first: float32 [512, 1024], P('dp')
- clipped_query_second: float32 [1024, 512], P('dp')
- clipped_query_third: float32 [512, 256], P('dp')
- clipped_item_first: float32 [512, 1024], P('dp')
- clipped_item_second: float32 [1024, 512], P('dp')
- clipped_item_third: float32 [512, 256], P('dp')
Inputs may be any that keep to these rules, and one draw needn't show every extreme that they name: `negative_ids`: ids of the sampled negatives; one id may stand for several negatives. `positive_ids`: A query's positive id may equal the ids of some negatives; those negatives are left out of that query's denominator.
All inputs are finite; a program needn't handle non-finite values.
Results may differ from a plain program's by a relative error of at most 0.0075.
Values may be sent and summed in bfloat16 or wider, within the bound.
A program may use at most 128 MiB of HBM per device.

v0:
```python
import jax
import jax.numpy as jnp
from jax import lax
from jax.sharding import PartitionSpec as P

inv_temp = 20.0
clip_norm = 256.0


def silu_slope(pre):
    sigma = jax.nn.sigmoid(pre)
    return sigma * (1.0 + pre * (1.0 - sigma))


def contract_rows(left, right):
    return lax.dot_general(
        left, right, (((0,), (0,)), ((), ())), preferred_element_type=jnp.float32
    )


def contract_cols(left, right):
    return lax.dot_general(
        left, right, (((1,), (1,)), ((), ())), preferred_element_type=jnp.float32
    )


def tower_forward(features, first, second, third):
    first_pre = jnp.dot(features, first, preferred_element_type=jnp.float32)
    first_act = jax.nn.silu(first_pre).astype(jnp.bfloat16)
    second_pre = jnp.dot(first_act, second, preferred_element_type=jnp.float32)
    second_act = jax.nn.silu(second_pre).astype(jnp.bfloat16)
    embedding = jnp.dot(second_act, third, preferred_element_type=jnp.float32)
    inv_norm = lax.rsqrt(jnp.sum(embedding * embedding, axis=1, keepdims=True) + 1.0)
    unit = (embedding * inv_norm).astype(jnp.bfloat16)
    return ((first_pre, first_act, second_pre, second_act, embedding, inv_norm), unit)


def tower_backward(features, second, third, saved, unit_grad):
    first_pre, first_act, second_pre, second_act, embedding, inv_norm = saved
    along = jnp.sum(embedding * unit_grad, axis=1, keepdims=True)
    embed_grad = (inv_norm * unit_grad - inv_norm * inv_norm * inv_norm * embedding * along).astype(
        jnp.bfloat16
    )
    third_grad = contract_rows(second_act, embed_grad)
    second_slope = (contract_cols(embed_grad, third) * silu_slope(second_pre)).astype(jnp.bfloat16)
    second_grad = contract_rows(first_act, second_slope)
    first_slope = (contract_cols(second_slope, second) * silu_slope(first_pre)).astype(jnp.bfloat16)
    first_grad = contract_rows(features, first_slope)
    return (first_grad, second_grad, third_grad)


def per_device(
    query_features,
    positive_features,
    negative_features,
    positive_ids,
    positive_counts,
    negative_ids,
    negative_counts,
    query_first,
    query_second,
    query_third,
    item_first,
    item_second,
    item_third,
):
    own_rows = query_features.shape[0]
    query_saved, query_unit = tower_forward(query_features, query_first, query_second, query_third)
    item_features = jnp.concatenate([positive_features, negative_features], axis=0)
    item_saved, item_unit = tower_forward(item_features, item_first, item_second, item_third)
    positive_unit = item_unit[:own_rows]
    negative_unit = item_unit[own_rows:]
    group_unit = lax.all_gather(query_unit, "neg", axis=0, tiled=True)
    shard_unit = lax.all_gather(negative_unit, "dp", axis=0, tiled=True)
    scores = (
        contract_cols(group_unit, shard_unit) * inv_temp
        - jnp.log(negative_counts.astype(jnp.float32))[None, :]
    )
    weights = jnp.where(positive_ids[:, None] != negative_ids[None, :], jnp.exp(scores), 0.0)
    positive_logit = jnp.sum(
        query_unit.astype(jnp.float32) * positive_unit.astype(jnp.float32), axis=1
    ) * inv_temp - jnp.log(positive_counts.astype(jnp.float32))
    positive_exp = jnp.exp(positive_logit)
    offset = lax.axis_index("neg") * own_rows
    partial_value = jnp.sum(weights, axis=1)
    own_part = lax.dynamic_slice(partial_value, (offset,), (own_rows,)) + positive_exp
    partial_value = lax.dynamic_update_slice(partial_value, own_part, (offset,))
    denom = lax.psum(partial_value, "neg")
    own_denom = lax.dynamic_slice(denom, (offset,), (own_rows,))
    loss_part = jnp.sum(jnp.log(own_denom) - positive_logit)
    softmax_weights = (weights / denom[:, None]).astype(jnp.bfloat16)
    positive_slope = positive_exp / own_denom - 1.0
    block = softmax_weights
    query_sum = lax.psum_scatter(
        jnp.dot(block, shard_unit, preferred_element_type=jnp.float32),
        "neg",
        scatter_dimension=0,
        tiled=True,
    )
    query_grad = (
        query_sum + positive_slope[:, None] * positive_unit.astype(jnp.float32)
    ) * inv_temp
    block = softmax_weights
    negative_sum = lax.psum_scatter(
        contract_rows(block, group_unit), "dp", scatter_dimension=0, tiled=True
    )
    positive_grad = positive_slope[:, None] * query_unit.astype(jnp.float32) * inv_temp
    item_grad = jnp.concatenate([positive_grad, negative_sum * inv_temp], axis=0)
    query_grads = tower_backward(query_features, query_second, query_third, query_saved, query_grad)
    item_grads = tower_backward(item_features, item_second, item_third, item_saved, item_grad)
    gradients = query_grads + item_grads
    loss_sum = lax.psum(loss_part, ("dp", "neg"))
    mean_loss = loss_sum / (own_rows * lax.axis_size("dp") * lax.axis_size("neg"))
    vectors = tuple((gradient.reshape(-1) for gradient in gradients))
    pieces = (
        lax.psum_scatter(vectors[0], ("dp", "neg"), scatter_dimension=0, tiled=True),
        lax.psum_scatter(vectors[1], ("dp", "neg"), scatter_dimension=0, tiled=True),
        lax.psum_scatter(vectors[2], ("dp", "neg"), scatter_dimension=0, tiled=True),
        lax.psum_scatter(vectors[3], ("dp", "neg"), scatter_dimension=0, tiled=True),
        lax.psum_scatter(vectors[4], ("dp", "neg"), scatter_dimension=0, tiled=True),
        lax.psum_scatter(vectors[5], ("dp", "neg"), scatter_dimension=0, tiled=True),
    )
    squares = jnp.zeros((), jnp.float32)
    for piece in pieces:
        squares = squares + jnp.sum(piece * piece)
    grad_norm = jnp.sqrt(lax.psum(squares, ("dp", "neg")))
    clip_factor = clip_norm / jnp.maximum(grad_norm, clip_norm)
    scaled = tuple((piece * clip_factor for piece in pieces))
    gathered = (
        lax.all_gather(scaled[0], "neg", axis=0, tiled=True),
        lax.all_gather(scaled[1], "neg", axis=0, tiled=True),
        lax.all_gather(scaled[2], "neg", axis=0, tiled=True),
        lax.all_gather(scaled[3], "neg", axis=0, tiled=True),
        lax.all_gather(scaled[4], "neg", axis=0, tiled=True),
        lax.all_gather(scaled[5], "neg", axis=0, tiled=True),
    )
    clipped = tuple(
        (vector.reshape(-1, gradient.shape[1]) for vector, gradient in zip(gathered, gradients))
    )
    return (mean_loss, clipped[0], clipped[1], clipped[2], clipped[3], clipped[4], clipped[5])


def solution(mesh):
    placed = (
        P(("dp", "neg"), None),
        P(("dp", "neg"), None),
        P(("neg", "dp"), None),
        P("dp"),
        P(("dp", "neg")),
        P("neg"),
        P("neg"),
        P(),
        P(),
        P(),
        P(),
        P(),
        P(),
    )
    return jax.shard_map(
        per_device,
        mesh=mesh,
        in_specs=placed,
        out_specs=(
            P(),
            P("dp", None),
            P("dp", None),
            P("dp", None),
            P("dp", None),
            P("dp", None),
            P("dp", None),
        ),
        check_vma=False,
    )
```

profile of v0, /device:TPU:0, one launch (start us, length us, event | category | flops | bytes accessed | tf_op | source)
XLA Modules:
  0.0 522.5 jit_solution(4157057472190406445)
XLA Ops:
  9.4 2.9 multiply_convert_fusion.1
  12.3 2.3 multiply_convert_fusion.3
  17.3 2.9 multiply_convert_fusion.6
  21.0 8.6 %all_gather.24 = bf16[1024,256]{0,1:T(8,128)(2,1)S(1)} all-gather(bf16[256,256]{0,1:T(8,128)(2,1)S(1)} %get-tuple-element.16), channel_id=1, replica_groups=mesh['dp'=8,'neg'=4] {'neg'}, dimensions={0}, use_global_device_ids=true | all-gather | bytes 655360 | tf_op jit(solution)/shard_map/all_gather | solution.py:73
  29.6 40.3 %all-gather.2.cloned.1.call-done = bf16[4096,256]{0,1:T(8,128)(2,1)} async-done(((bf16[512,256]{0,1:T(8,128)(2,1)}), bf16[4096,256]{0,1:T(8,128)(2,1)}) %all-gather.2.cloned.1.call-update) | async-done | bytes 2097168 | tf_op jit(solution)/shard_map/all_gather | solution.py:74
  70.0 9.7 %fusion = (f32[1024]{0:T(1024)S(1)}, f32[1024,4096]{1,0:T(8,128)}) fusion(f32[4096]{0:T(1024)S(1)} %convert_log_fusion, s32[4096]{0:T(1024)S(1)} %copy-done.18, s32[1024]{0:T(1024)S(1)} %copy-done.19, bf16[1024,256]{0,1:T(8,128)(2,1)S(1)} %all_gather.24, bf16[4096,256]{0,1:T(8,128)(2,1)} %all-gather.2.cloned.1.call-done), kind=kOutput, calls=%fused_computation.2 | convolution fusion | flops 2168454144 | bytes 19439616 | tf_op jit(solution)/shard_map/dot_general | solution.py:22
  79.8 5.8 %psum.21 = f32[1024]{0:T(1024)S(1)} all-reduce(f32[1024]{0:T(1024)S(1)} %add_dynamic-update-slice_fusion), channel_id=1, replica_groups=mesh['dp'=8,'neg'=4] {'neg'}, use_global_device_ids=true, to_apply=%region_4.5 | all-reduce | flops 1024 | bytes 8192 | tf_op jit(solution)/shard_map/psum | solution.py:88
  85.6 8.4 %divide_convert_fusion = bf16[1024,4096]{1,0:T(8,128)(2,1)S(1)} fusion(f32[1024,4096]{1,0:T(8,128)} %get-tuple-element.37, f32[1024]{0:T(1024)S(1)} %psum.21, f32[4096]{0:T(1024)S(1)} %convert_log_fusion, s32[4096]{0:T(1024)S(1)} %copy-done.18, s32[1024]{0:T(1024)S(1)} %copy-done.19), kind=kLoop, calls=%fused_computation | loop fusion | flops 25165824 | bytes 25206784 | tf_op jit(solution)/shard_map/convert_element_type | solution.py:91
  94.0 3.2 copy-done.2
  97.2 3.3 fusion.15
  100.8 7.7 %fusion.16 = f32[4096,256]{0,1:T(8,128)} fusion(bf16[1024,256]{0,1:T(8,128)(2,1)S(1)} %all_gather.24, bf16[1024,4096]{1,0:T(8,128)(2,1)} %copy-done.2), kind=kOutput, calls=%fused_computation.73 | convolution fusion | flops 2147483648 | bytes 13107200 | tf_op jit(solution)/shard_map/dot_general | solution.py:16
  109.2 14.5 %reduce-scatter.3.cloned.1.call-done = f32[256,256]{0,1:T(8,128)} async-done(((f32[1024,256]{0,1:T(8,128)}), f32[256,256]{0,1:T(8,128)}) %reduce-scatter.3.cloned.1.call-update) | async-done | bytes 262160 | tf_op jit(solution)/shard_map/reduce_scatter | solution.py:94
  125.9 1.4 fusion.2
  127.3 3.5 convolution_bitcast_fusion.1
  130.8 1.9 copy.26
  132.7 1.8 copy.30
  135.1 1.9 copy.31
  138.3 77.8 %reduce-scatter.5.cloned.1.call-done = f32[512,256]{0,1:T(8,128)} async-done(((f32[4096,256]{0,1:T(8,128)}), f32[512,256]{0,1:T(8,128)}) %reduce-scatter.5.cloned.1.call-update) | async-done | bytes 524304 | tf_op jit(solution)/shard_map/reduce_scatter | solution.py:104
  221.7 1.9 copy.34
  223.6 4.5 convolution_bitcast_fusion.3
  228.1 1.8 copy.33
  229.9 191.2 %all-reduce.10.cloned.1.call-done = (f32[524288]{0:T(1024)}, f32[524288]{0:T(1024)}, f32[131072]{0:T(1024)}, f32[524288]{0:T(1024)}, f32[524288]{0:T(1024)}, /*index=5*/f32[131072]{0:T(1024)}) async-done(((f32[524288]{0:T(1024)}, f32[524288]{0:T(1024)}, f32[131072]{0:T(1024)}, f32[524288]{0:T(1024)}, f32[524288]{0:T(1024)}, /*index=5*/f32[131072]{0:T(1024)}), (f32[524288]{0:T(1024)}, f32[524288]{0:T(1024)}, ...) | async-done | bytes 9437200
  421.1 1.5 multiply_reduce_fusion.4
  422.6 1.5 multiply_reduce_fusion.6
  425.4 1.4 multiply_reduce_fusion.8
  429.4 40.4 %all-reduce.6 = (f32[]{:T(128)}, f32[]{:T(128)}) all-reduce(f32[]{:T(128)} %get-tuple-element.18, f32[]{:T(128)S(6)} %add.128), channel_id=1, replica_groups=mesh['dp'=8,'neg'=4] {'dp','neg'}, use_global_device_ids=true, to_apply=%region_6.7 | all-reduce | flops 2 | bytes 16 | tf_op jit(solution)/shard_map/psum | solution.py:112
  475.5 5.5 %all_gather.31 = f32[16384]{0:T(1024)S(1)} all-gather(f32[4096]{0:T(1024)S(1)} %dynamic-slice_multiply_fusion.4), channel_id=1, replica_groups=mesh['dp'=8,'neg'=4] {'neg'}, dimensions={0}, use_global_device_ids=true | all-gather | bytes 81920 | tf_op jit(solution)/shard_map/all_gather | solution.py:135
  481.6 6.3 %all_gather.30 = f32[65536]{0:T(1024)S(1)} all-gather(f32[16384]{0:T(1024)S(1)} %dynamic-slice_multiply_fusion), channel_id=1, replica_groups=mesh['dp'=8,'neg'=4] {'neg'}, dimensions={0}, use_global_device_ids=true | all-gather | bytes 327680 | tf_op jit(solution)/shard_map/all_gather | solution.py:134
  488.6 5.8 %all_gather.29 = f32[65536]{0:T(1024)S(1)} all-gather(f32[16384]{0:T(1024)S(1)} %dynamic-slice_multiply_fusion.1), channel_id=1, replica_groups=mesh['dp'=8,'neg'=4] {'neg'}, dimensions={0}, use_global_device_ids=true | all-gather | bytes 327680 | tf_op jit(solution)/shard_map/all_gather | solution.py:133
  495.2 5.2 all_gather.28
  501.0 5.8 %all_gather.27 = f32[65536]{0:T(1024)S(1)} all-gather(f32[16384]{0:T(1024)S(1)} %dynamic-slice_multiply_fusion.2), channel_id=1, replica_groups=mesh['dp'=8,'neg'=4] {'neg'}, dimensions={0}, use_global_device_ids=true | all-gather | bytes 327680 | tf_op jit(solution)/shard_map/all_gather | solution.py:131
  507.6 5.8 %all_gather.26 = f32[65536]{0:T(1024)S(1)} all-gather(f32[16384]{0:T(1024)S(1)} %dynamic-slice_multiply_fusion.3), channel_id=1, replica_groups=mesh['dp'=8,'neg'=4] {'neg'}, dimensions={0}, use_global_device_ids=true | all-gather | bytes 327680 | tf_op jit(solution)/shard_map/all_gather | solution.py:130
  (98 shorter events, 25.5 us)
Async XLA Ops:
  7.2 2.2 copy-start
  7.2 62.8 %all-gather.2.cloned.1.call-start = ((), (), s32[]{:S(2)}) async-start(), calls=%async_computation.2 | async-start | bytes 2359296 | tf_op jit(solution)/shard_map/all_gather | solution.py:74
  9.4 2.9 copy-start.15
  9.4 2.9 copy-start.22
  12.3 2.3 copy-start.23
  12.3 3.2 copy-start.12
  14.6 0.9 copy-start.3
  14.6 2.2 copy-start.7
  14.6 2.2 copy-start.11
  16.7 107.0 %reduce-scatter.3.cloned.1.call-start = ((), (), s32[]{:S(2)}) async-start(), calls=%async_computation.3 | async-start | bytes 1310720 | tf_op jit(solution)/shard_map/reduce_scatter | solution.py:94
  17.2 3.0 copy-start.8
  17.2 3.0 copy-start.14
  17.3 12.3 %copy-start.17 = (s32[4096]{0:T(1024)S(1)}, s32[4096]{0:T(1024)}, u32[]{:S(2)}) copy-start(s32[4096]{0:T(1024)} %param.19) | copy-start | bytes 49156
  17.3 52.7 %copy-start.18 = (s32[4096]{0:T(1024)S(1)}, s32[4096]{0:T(1024)}, u32[]{:S(2)}) copy-start(s32[4096]{0:T(1024)} %param.18) | copy-start | bytes 49156
  17.3 52.7 %copy-start.19 = (s32[1024]{0:T(1024)S(1)}, s32[1024]{0:T(1024)}, u32[]{:S(2)}) copy-start(s32[1024]{0:T(1024)} %param.16) | copy-start | bytes 12292
  20.2 0.7 copy-start.5
  29.6 50.0 %copy-start.20 = (s32[256]{0:T(256)S(1)}, s32[256]{0:T(256)}, u32[]{:S(2)}) copy-start(s32[256]{0:T(256)} %param.17) | copy-start | bytes 3076
  85.6 11.6 %copy-start.21 = (bf16[4096,256]{0,1:T(8,128)(2,1)S(1)}, bf16[4096,256]{0,1:T(8,128)(2,1)}, u32[]{:S(2)}) copy-start(bf16[4096,256]{0,1:T(8,128)(2,1)} %all-gather.2.cloned.1.call-done) | copy-start | bytes 6291460
  94.0 3.2 copy-start.2
  100.6 115.6 %reduce-scatter.5.cloned.1.call-start = ((), (), s32[]{:S(2)}) async-start(), calls=%async_computation.4 | async-start | bytes 4718592 | tf_op jit(solution)/shard_map/reduce_scatter | solution.py:104
  108.5 312.6 %all-reduce.10.cloned.1.call-start = ((), (), s32[]{:S(2)}) async-start(), calls=%async_computation.5 | async-start | bytes 18874368
  124.8 2.5 copy-start.9
  132.7 1.8 copy-start.10
  135.0 1.9 copy-start.6
  138.3 79.2 %copy-start.4 = (bf16[768,512]{1,0:T(8,128)(2,1)S(1)}, bf16[768,512]{1,0:T(8,128)(2,1)}, u32[]{:S(2)}) copy-start(bf16[768,512]{1,0:T(8,128)(2,1)} %copy-done.3) | copy-start | bytes 2359300
  217.3 1.7 copy-start.13
  217.3 1.7 copy-start.26
  219.1 1.6 copy-start.24
  219.8 0.9 copy-start.25
  221.7 1.9 copy-start.16
  472.1 42.7 %copy-start.1 = (bf16[512,1024]{1,0:T(8,128)(2,1)S(1)}, bf16[512,1024]{1,0:T(8,128)(2,1)}, u32[]{:S(2)}) copy-start(bf16[512,1024]{1,0:T(8,128)(2,1)} %param.23) | copy-start | bytes 3145732
Sparse Core Ops, SparseCore 0:
  16.8 53.0 all-gather.1
  100.7 23.0 reduce-scatter.2
  127.4 88.6 reduce-scatter.4
  230.0 191.0 all-reduce.9
where the time goes:
time: 524 us; the launch traced here: 523 us
  waiting for transfers between devices  324 us (62%)
  blocking collectives  89.4 us (17%)
  matrix products  42.1 us (8%)
  local copies, waits for them, and re-layouts  24.1 us (5%)
  other arithmetic  22.1 us (4%)
  between operations  20.5 us (4%)
    unnamed x5, waiting for transfers between devices  191 us
    reduce_scatter x1, waiting for transfers between devices, per_device(): lax.psum_scatter(contract_rows(block, group_unit), 'dp', scatter_dimensio...  77.8 us
    psum x1, blocking collectives, per_device(): loss_sum = lax.psum(loss_part, ('dp', 'neg'))  40.4 us
    all_gather x1, waiting for transfers between devices, per_device(): shard_unit = lax.all_gather(negative_unit, 'dp', axis=0, tiled=True)  40.3 us
    dot_general x7, matrix products, contract_rows(): lax.dot_general(left, right, (((0,), (0,)), ((), ())), preferred_element_...  17.9 us
    unnamed x61, local copies, waits for them, and re-layouts  16.1 us
    reduce_scatter x1, waiting for transfers between devices, per_device(): lax.psum_scatter(jnp.dot(block, shard_unit, preferred_element_type=jnp.fl...  14.5 us
    dot_general x3, matrix products, contract_cols(): lax.dot_general(left, right, (((1,), (1,)), ((), ())), preferred_element_...  11.7 us
  transfers between devices with their start and end apart: 4, of which 4 were waited for; matrix products, arithmetic and copies ran while one was open for 5% of the time, Pallas kernels for 0%

commit v1 on v0

--- a/solution.py
+++ b/solution.py
@@ -71,7 +71,14 @@
     positive_unit = item_unit[:own_rows]
     negative_unit = item_unit[own_rows:]
     group_unit = lax.all_gather(query_unit, "neg", axis=0, tiled=True)
-    shard_unit = lax.all_gather(negative_unit, "dp", axis=0, tiled=True)
+    ways, here, lap = (lax.axis_size("dp"), lax.axis_index("dp"), negative_unit.shape[0])
+    line, have = (negative_unit, 1)
+    while have < ways:
+        line = jnp.concatenate(
+            [line, lax.ppermute(line, "dp", [(d, (d - have) % ways) for d in range(ways)])], axis=0
+        )
+        have = 2 * have
+    shard_unit = jnp.roll(line, here * lap, axis=0)
     scores = (
         contract_cols(group_unit, shard_unit) * inv_temp
         - jnp.log(negative_counts.astype(jnp.float32))[None, :]

time: 524 us -> 543 us (1.036)
  waiting for transfers between devices: 324 us -> 339 us
  starting transfers between devices: 0.34 us -> 8.49 us
    ppermute x0 -> x3, waiting for transfers between devices: none -> 52.2 us  [per_device(): lax.ppermute(line, 'dp', [(d, (d - have) % ways) for d in range(ways)])]
    all_gather x1 -> x0, waiting for transfers between devices: 40.3 us -> none  [per_device(): shard_unit = lax.all_gather(negative_unit, 'dp', axis=0, tiled=True)]
    ppermute x0 -> x3, starting transfers between devices: none -> 8.19 us  [per_device(): lax.ppermute(line, 'dp', [(d, (d - have) % ways) for d in range(ways)])]
    unnamed x61 -> x75, local copies, waits for them, and re-layouts: 16.1 us -> 15.7 us
    unnamed x5 -> x4, waiting for transfers between devices: 191 us -> 191 us
  transfers between devices with their start and end apart: 4 -> 6, of which waited for: 4 -> 6; matrix products, arithmetic and copies ran while one was open for 5% -> 5% of each run, Pallas kernels for 0% -> 0%
where the time goes in v1:
time: 543 us; the launch traced here: 542 us
  waiting for transfers between devices  339 us (62%)
  blocking collectives  88.1 us (16%)
  matrix products  39.2 us (7%)
  local copies, waits for them, and re-layouts  23.9 us (4%)
  other arithmetic  22.8 us (4%)
  between operations  20.6 us (4%)
  starting transfers between devices  8.49 us (2%)
    unnamed x4, waiting for transfers between devices  191 us
    reduce_scatter x1, waiting for transfers between devices, per_device(): lax.psum_scatter(contract_rows(block, group_unit), 'dp', scatter_dimensio...  77.8 us
    ppermute x3, waiting for transfers between devices, per_device(): lax.ppermute(line, 'dp', [(d, (d - have) % ways) for d in range(ways)])  52.2 us
    psum x1, blocking collectives, per_device(): loss_sum = lax.psum(loss_part, ('dp', 'neg'))  40.5 us
    reduce_scatter x1, waiting for transfers between devices, per_device(): lax.psum_scatter(jnp.dot(block, shard_unit, preferred_element_type=jnp.fl...  18 us
    dot_general x7, matrix products, contract_rows(): lax.dot_general(left, right, (((0,), (0,)), ((), ())), preferred_element_...  17.9 us
    unnamed x75, local copies, waits for them, and re-layouts  15.7 us
  transfers between devices with their start and end apart: 6, of which 6 were waited for; matrix products, arithmetic and copies ran while one was open for 5% of the time, Pallas kernels for 0%

profile of v1, /device:TPU:0, one launch (start us, length us, event | category | flops | bytes accessed | tf_op | source)
XLA Modules:
  0.0 542.3 jit_solution(18061602306348163416)
XLA Ops:
  9.4 2.9 multiply_convert_fusion.1
  12.3 2.3 multiply_convert_fusion.3
  15.9 6.0 %collective-permute-start = (bf16[512,256]{0,1:T(8,128)(2,1)S(1)}, bf16[512,256]{0,1:T(8,128)(2,1)S(1)}, u32[]{:S(2)}, u32[]{:S(2)}) collective-permute-start(bf16[512,256]{0,1:T(8,128)(2,1)S(1)} %get-tuple-element.17), channel_id=1, source_target_pairs={{0,28},{4,0},{8,4},{12,8},{16,12},{20,16},{24,20},{28,24},{1,29},{... | collective-permute-start | bytes 786440 | tf_op jit(solution)/shard_map/ppermute | solution.py:78
  22.4 5.1 collective-permute-done
  27.6 1.6 collective-permute-start.1
  31.4 9.0 %collective-permute-done.1 = bf16[1024,256]{0,1:T(8,128)(2,1)S(1)} collective-permute-done((bf16[1024,256]{0,1:T(8,128)(2,1)S(1)}, bf16[1024,256]{0,1:T(8,128)(2,1)S(1)}, u32[]{:S(2)}, u32[]{:S(2)}) %collective-permute-start.1) | collective-permute-done | bytes 524320 | tf_op jit(solution)/shard_map/ppermute | solution.py:78
  41.8 7.2 %all_gather.21 = bf16[1024,256]{0,1:T(8,128)(2,1)S(1)} all-gather(bf16[256,256]{0,1:T(8,128)(2,1)S(1)} %get-tuple-element.16), channel_id=1, replica_groups=mesh['dp'=8,'neg'=4] {'neg'}, dimensions={0}, use_global_device_ids=true | all-gather | bytes 655360 | tf_op jit(solution)/shard_map/all_gather | solution.py:73
  49.0 38.1 %collective-permute-done.2 = bf16[2048,256]{0,1:T(8,128)(2,1)S(1)} collective-permute-done((bf16[2048,256]{0,1:T(8,128)(2,1)S(1)}, bf16[2048,256]{0,1:T(8,128)(2,1)S(1)}, u32[]{:S(2)}, u32[]{:S(2)}) %collective-permute-start.2) | collective-permute-done | bytes 1048608 | tf_op jit(solution)/shard_map/ppermute | solution.py:78
  87.5 8.2 %fusion = (f32[1024]{0:T(1024)S(1)}, f32[1024,4096]{1,0:T(8,128)}) fusion(f32[4096]{0:T(1024)S(1)} %convert_log_fusion, s32[4096]{0:T(1024)S(1)} %copy-done.22, s32[1024]{0:T(1024)S(1)} %copy-done.23, bf16[1024,256]{0,1:T(8,128)(2,1)S(1)} %all_gather.21, bf16[8192,256]{0,1:T(8,128)(2,1)S(1)} %constant_dynamic-update-slice_fusion.2, s32[]{:T(128)S(6)} %select_n.23), kind=kOutput, calls=%fused_computation.2 | convolution fusion | flops 2168454144 | bytes 19439620 | tf_op jit(solution)/shard_map/dot_general | solution.py:22
  95.8 6.0 %psum.21 = f32[1024]{0:T(1024)S(1)} all-reduce(f32[1024]{0:T(1024)S(1)} %add_dynamic-update-slice_fusion), channel_id=1, replica_groups=mesh['dp'=8,'neg'=4] {'neg'}, use_global_device_ids=true, to_apply=%region_4.5 | all-reduce | flops 1024 | bytes 8192 | tf_op jit(solution)/shard_map/psum | solution.py:95
  101.9 8.5 %divide_convert_fusion = bf16[1024,4096]{1,0:T(8,128)(2,1)S(1)} fusion(f32[1024,4096]{1,0:T(8,128)} %get-tuple-element.39, f32[1024]{0:T(1024)S(1)} %psum.21, f32[4096]{0:T(1024)S(1)} %convert_log_fusion, s32[4096]{0:T(1024)S(1)} %copy-done.22, s32[1024]{0:T(1024)S(1)} %copy-done.23), kind=kLoop, calls=%fused_computation | loop fusion | flops 25165824 | bytes 25206784 | tf_op jit(solution)/shard_map/convert_element_type | solution.py:98
  110.4 3.2 copy-done.2
  113.6 3.4 fusion.1
  117.3 7.7 %fusion.22 = f32[4096,256]{0,1:T(8,128)} fusion(bf16[1024,256]{0,1:T(8,128)(2,1)S(1)} %all_gather.21, bf16[1024,4096]{1,0:T(8,128)(2,1)} %copy-done.2), kind=kOutput, calls=%fused_computation.89 | convolution fusion | flops 2147483648 | bytes 13107200 | tf_op jit(solution)/shard_map/dot_general | solution.py:16
  125.8 18.0 %reduce-scatter.3.cloned.1.call-done = f32[256,256]{0,1:T(8,128)} async-done(((f32[1024,256]{0,1:T(8,128)}), f32[256,256]{0,1:T(8,128)}) %reduce-scatter.3.cloned.1.call-update) | async-done | bytes 262160 | tf_op jit(solution)/shard_map/reduce_scatter | solution.py:101
  147.2 3.5 convolution_bitcast_fusion.1
  150.7 1.9 copy.26
  152.6 1.8 copy.30
  154.9 1.9 copy.31
  158.2 77.8 %reduce-scatter.5.cloned.1.call-done = f32[512,256]{0,1:T(8,128)} async-done(((f32[4096,256]{0,1:T(8,128)}), f32[512,256]{0,1:T(8,128)}) %reduce-scatter.5.cloned.1.call-update) | async-done | bytes 524304 | tf_op jit(solution)/shard_map/reduce_scatter | solution.py:111
  241.6 1.9 copy.34
  243.4 4.5 convolution_bitcast_fusion.3
  248.0 1.8 copy.33
  249.8 191.2 %all-reduce.10.cloned.1.call-done = (f32[524288]{0:T(1024)}, f32[524288]{0:T(1024)}, f32[131072]{0:T(1024)}, f32[524288]{0:T(1024)}, f32[524288]{0:T(1024)}, /*index=5*/f32[131072]{0:T(1024)}) async-done(((f32[524288]{0:T(1024)}, f32[524288]{0:T(1024)}, f32[131072]{0:T(1024)}, f32[524288]{0:T(1024)}, f32[524288]{0:T(1024)}, /*index=5*/f32[131072]{0:T(1024)}), (f32[524288]{0:T(1024)}, f32[524288]{0:T(1024)}, ...) | async-done | bytes 9437200
  441.0 1.5 multiply_reduce_fusion.4
  449.2 40.5 %all-reduce.6 = (f32[]{:T(128)}, f32[]{:T(128)}) all-reduce(f32[]{:T(128)} %get-tuple-element.20, f32[]{:T(128)S(6)} %add.140), channel_id=1, replica_groups=mesh['dp'=8,'neg'=4] {'dp','neg'}, use_global_device_ids=true, to_apply=%region_6.7 | all-reduce | flops 2 | bytes 16 | tf_op jit(solution)/shard_map/psum | solution.py:119
  495.3 5.5 %all_gather.27 = f32[16384]{0:T(1024)S(1)} all-gather(f32[4096]{0:T(1024)S(1)} %dynamic-slice_multiply_fusion.4), channel_id=1, replica_groups=mesh['dp'=8,'neg'=4] {'neg'}, dimensions={0}, use_global_device_ids=true | all-gather | bytes 81920 | tf_op jit(solution)/shard_map/all_gather | solution.py:142
  501.4 6.3 %all_gather.26 = f32[65536]{0:T(1024)S(1)} all-gather(f32[16384]{0:T(1024)S(1)} %dynamic-slice_multiply_fusion), channel_id=1, replica_groups=mesh['dp'=8,'neg'=4] {'neg'}, dimensions={0}, use_global_device_ids=true | all-gather | bytes 327680 | tf_op jit(solution)/shard_map/all_gather | solution.py:141
  508.4 5.8 %all_gather.25 = f32[65536]{0:T(1024)S(1)} all-gather(f32[16384]{0:T(1024)S(1)} %dynamic-slice_multiply_fusion.1), channel_id=1, replica_groups=mesh['dp'=8,'neg'=4] {'neg'}, dimensions={0}, use_global_device_ids=true | all-gather | bytes 327680 | tf_op jit(solution)/shard_map/all_gather | solution.py:140
  515.0 5.2 all_gather.24
  520.8 5.8 %all_gather.23 = f32[65536]{0:T(1024)S(1)} all-gather(f32[16384]{0:T(1024)S(1)} %dynamic-slice_multiply_fusion.2), channel_id=1, replica_groups=mesh['dp'=8,'neg'=4] {'neg'}, dimensions={0}, use_global_device_ids=true | all-gather | bytes 327680 | tf_op jit(solution)/shard_map/all_gather | solution.py:138
  527.4 5.8 %all_gather.22 = f32[65536]{0:T(1024)S(1)} all-gather(f32[16384]{0:T(1024)S(1)} %dynamic-slice_multiply_fusion.3), channel_id=1, replica_groups=mesh['dp'=8,'neg'=4] {'neg'}, dimensions={0}, use_global_device_ids=true | all-gather | bytes 327680 | tf_op jit(solution)/shard_map/all_gather | solution.py:137
  (118 shorter events, 31.8 us)
Async XLA Ops:
  7.2 2.2 copy-start
  7.2 136.5 %reduce-scatter.3.cloned.1.call-start = ((), (), s32[]{:S(2)}) async-start(), calls=%async_computation.2 | async-start | bytes 1310720 | tf_op jit(solution)/shard_map/reduce_scatter | solution.py:101
  9.4 2.9 copy-start.16
  9.4 2.9 copy-start.26
  12.3 2.3 copy-start.27
  12.3 2.3 copy-start.13
  14.6 7.3 %copy-start.7 = (bf16[512,1024]{1,0:T(8,128)(2,1)S(1)}, bf16[512,1024]{1,0:T(8,128)(2,1)}, u32[]{:S(2)}) copy-start(bf16[512,1024]{1,0:T(8,128)(2,1)} %param.20) | copy-start | bytes 3145732
  14.6 7.3 %copy-start.11 = (bf16[256,512]{1,0:T(8,128)(2,1)S(1)}, bf16[256,512]{1,0:T(8,128)(2,1)}, u32[]{:S(2)}) copy-start(bf16[256,512]{1,0:T(8,128)(2,1)} %param.13) | copy-start | bytes 786436
  15.9 11.6 %collective-permute-start = (bf16[512,256]{0,1:T(8,128)(2,1)S(1)}, bf16[512,256]{0,1:T(8,128)(2,1)S(1)}, u32[]{:S(2)}, u32[]{:S(2)}) collective-permute-start(bf16[512,256]{0,1:T(8,128)(2,1)S(1)} %get-tuple-element.17), channel_id=1, source_target_pairs={{0,28},{4,0},{8,4},{12,8},{16,12},{20,16},{24,20},{28,24},{1,29},{... | collective-permute-start | bytes 786440 | tf_op jit(solution)/shard_map/ppermute | solution.py:78
  21.9 7.2 %copy-start.25 = (bf16[1024,512]{1,0:T(8,128)(2,1)S(1)}, bf16[1024,512]{1,0:T(8,128)(2,1)}, u32[]{:S(2)}) copy-start(bf16[1024,512]{1,0:T(8,128)(2,1)} %param.21) | copy-start | bytes 3145732
  22.4 8.1 %copy-start.8 = (f32[256,1024]{1,0:T(8,128)}, f32[256,1024]{1,0:T(8,128)S(1)}, u32[]{:S(2)}) copy-start(f32[256,1024]{1,0:T(8,128)S(1)} %fusion.21) | copy-start | bytes 3145732
  27.6 3.6 copy-start.15
  27.6 12.9 %collective-permute-start.1 = (bf16[1024,256]{0,1:T(8,128)(2,1)S(1)}, bf16[1024,256]{0,1:T(8,128)(2,1)S(1)}, u32[]{:S(2)}, u32[]{:S(2)}) collective-permute-start(bf16[1024,256]{0,1:T(8,128)(2,1)S(1)} %pad_maximum_fusion.2), channel_id=1, source_target_pairs={{0,24},{4,28},{8,0},{12,4},{16,8},{20,12},{24,16},{28,20},{1,25},{... | collective-permute-start | bytes 1572872 | tf_op jit(solution)/shard_map/ppermute | solution.py:78
  29.2 19.8 %copy-start.18 = (bf16[8192,256]{0,1:T(8,128)(2,1)S(1)}, bf16[8192,256]{0,1:T(8,128)(2,1)}, u32[]{:S(2)}) copy-start(bf16[8192,256]{0,1:T(8,128)(2,1)} %get-tuple-element.18) | copy-start | bytes 12582916
  30.4 18.5 %copy-start.21 = (s32[4096]{0:T(1024)S(1)}, s32[4096]{0:T(1024)}, u32[]{:S(2)}) copy-start(s32[4096]{0:T(1024)} %param.19) | copy-start | bytes 49156
  40.5 46.6 %collective-permute-start.2 = (bf16[2048,256]{0,1:T(8,128)(2,1)S(1)}, bf16[2048,256]{0,1:T(8,128)(2,1)S(1)}, u32[]{:S(2)}, u32[]{:S(2)}) collective-permute-start(bf16[2048,256]{0,1:T(8,128)(2,1)S(1)} %pad_maximum_fusion), channel_id=1, source_target_pairs={{0,16},{4,20},{8,24},{12,28},{16,0},{20,4},{24,8},{28,12},{1,17},{... | collective-permute-start | bytes 3145736 | tf_op jit(solution)/shard_map/ppermute | solution.py:78
  49.0 38.4 %copy-start.22 = (s32[4096]{0:T(1024)S(1)}, s32[4096]{0:T(1024)}, u32[]{:S(2)}) copy-start(s32[4096]{0:T(1024)} %param.18) | copy-start | bytes 49156
  49.0 38.4 %copy-start.23 = (s32[1024]{0:T(1024)S(1)}, s32[1024]{0:T(1024)}, u32[]{:S(2)}) copy-start(s32[1024]{0:T(1024)} %param.16) | copy-start | bytes 12292
  87.4 8.2 %copy-start.19 = (bf16[8192,256]{0,1:T(8,128)(2,1)}, bf16[8192,256]{0,1:T(8,128)(2,1)S(1)}, u32[]{:S(2)}) copy-start(bf16[8192,256]{0,1:T(8,128)(2,1)S(1)} %constant_dynamic-update-slice_fusion.2) | copy-start | bytes 12582916
  87.4 8.2 %copy-start.24 = (s32[256]{0:T(256)S(1)}, s32[256]{0:T(256)}, u32[]{:S(2)}) copy-start(s32[256]{0:T(256)} %param.17) | copy-start | bytes 3076
  101.9 11.8 %copy-start.20 = (bf16[8192,256]{0,1:T(8,128)(2,1)S(1)}, bf16[8192,256]{0,1:T(8,128)(2,1)}, u32[]{:S(2)}) copy-start(bf16[8192,256]{0,1:T(8,128)(2,1)} %copy-done.19) | copy-start | bytes 12582916
  110.4 3.2 copy-start.2
  117.1 119.0 %reduce-scatter.5.cloned.1.call-start = ((), (), s32[]{:S(2)}) async-start(), calls=%async_computation.3 | async-start | bytes 4718592 | tf_op jit(solution)/shard_map/reduce_scatter | solution.py:111
  125.0 22.2 %copy-start.9 = (f32[256,1024]{1,0:T(8,128)S(1)}, f32[256,1024]{1,0:T(8,128)}, u32[]{:S(2)}) copy-start(f32[256,1024]{1,0:T(8,128)} %copy-done.8) | copy-start | bytes 3145732
  125.0 22.2 %copy-start.12 = (bf16[256,512]{1,0:T(8,128)(2,1)S(1)}, bf16[256,512]{1,0:T(8,128)(2,1)}, u32[]{:S(2)}) copy-start(bf16[256,512]{1,0:T(8,128)(2,1)} %param.13) | copy-start | bytes 786436
  125.0 316.0 %all-reduce.10.cloned.1.call-start = ((), (), s32[]{:S(2)}) async-start(), calls=%async_computation.4 | async-start | bytes 18874368
  152.6 1.8 copy-start.10
  154.9 1.9 copy-start.6
  156.8 80.6 %copy-start.4 = (bf16[768,512]{1,0:T(8,128)(2,1)S(1)}, bf16[768,512]{1,0:T(8,128)(2,1)}, u32[]{:S(2)}) copy-start(bf16[768,512]{1,0:T(8,128)(2,1)} %copy-done.3) | copy-start | bytes 2359300
  237.1 1.8 copy-start.14
  241.6 1.9 copy-start.17
  249.8 284.9 %copy-start.1 = (bf16[512,1024]{1,0:T(8,128)(2,1)S(1)}, bf16[512,1024]{1,0:T(8,128)(2,1)}, u32[]{:S(2)}) copy-start(bf16[512,1024]{1,0:T(8,128)(2,1)} %param.23) | copy-start | bytes 3145732
  (5 other events, 6.4 us)
Sparse Core Ops, SparseCore 0:
  117.2 26.4 reduce-scatter.2
  147.3 88.6 reduce-scatter.4
  249.9 191.0 all-reduce.9
